TPU v7x, 32 devices: a whole 2x2x4 slice. The times are simulated.
32 devices in a mesh: dp: 8 (over z, y), fsdp: 4 (over x, core).
Axes of the slice: x: 2, y: 2, z: 4, core: 2. Of those that a mesh axis runs over, the one named last changes fastest.
Arguments:
- momentum: float32 [2, 6144, 16384], P(None, 'fsdp', 'dp'), may hold values from -160 to 160, as said below
- gradient: bfloat16 [2, 6144, 16384], P(None, 'fsdp', 'dp'), may hold values from -6 to 6
- q_factor: float32 [2, 16384, 256], P(None, 'dp'), may hold values from -6 to 6
Outputs:
- new_momentum: float32 [2, 6144, 16384], P(None, 'fsdp', 'dp')
- update: bfloat16 [2, 6144, 16384], P(None, 'fsdp', 'dp')
- new_q: float32 [2, 16384, 256], P(None, 'dp')
Inputs may be any that keep to these rules, and one draw needn't show every extreme that they name: `momentum`: Real-valued entries.
All inputs are finite; a program needn't handle non-finite values.
Results may differ from a plain program's by a relative error of at most 0.001.
Values sent between devices are 32-bit elements; how exact they have to be, the bound alone decides.
A program may use at most 192 MiB of HBM per device.

v0:
```python
import functools
import math

import jax
import jax.numpy as jnp
from jax import lax
from jax.experimental import pallas as pl
from jax.experimental.pallas import tpu as pltpu
from jax.sharding import PartitionSpec as P

MESH = pl.DeviceIdType.MESH
F32 = jnp.float32
BF16 = jnp.bfloat16

ema_decay = 0.75
epsilon = 1e-06
BLOCK = 128
FULL = lax.Precision.HIGHEST
THREE = lax.Precision.HIGH
ONE = lax.Precision.DEFAULT


def inverse_factor_kernel(gram_ref, out_ref, work_left, work_right):
    matrices, size, _ = gram_ref.shape
    rows = lax.broadcasted_iota(jnp.int32, (size, 1), 0)
    lanes = lax.broadcasted_iota(jnp.int32, (1, size), 1)
    eye = jnp.where(rows == lanes, 1.0, 0.0).astype(jnp.float32)
    for e in range(matrices):
        work_left[e] = gram_ref[e]
        work_right[e] = eye

    def step(k, carry):
        for e in range(matrices):
            left = work_left[e]
            right = work_right[e]
            row_left = work_left[e, pl.ds(k, 1), :]
            row_right = work_right[e, pl.ds(k, 1), :]
            pivot = jnp.sum(jnp.where(lanes == k, row_left, 0.0), axis=1, keepdims=True)
            inverse = lax.rsqrt(pivot)
            row_left = row_left * inverse
            row_right = row_right * inverse
            column = jnp.sum(jnp.where(lanes == k, left, 0.0), axis=1, keepdims=True)
            column = jnp.where(rows > k, column * inverse, 0.0)
            work_left[e] = left - column * row_left
            work_right[e] = jnp.where(rows == k, row_right, right - column * row_right)
        return carry

    lax.fori_loop(0, size, step, 0)
    for e in range(matrices):
        out_ref[e] = work_right[e]


def inverse_factor(gram):
    matrices, size, _ = gram.shape
    if size > BLOCK:
        half = size // 2
        top = inverse_factor(gram[:, :half, :half])
        low = jnp.einsum("eij,ekj->eik", gram[:, half:, :half], top, precision=FULL)
        rest = gram[:, half:, half:] - jnp.einsum("eij,ekj->eik", low, low, precision=FULL)
        bottom = inverse_factor(rest)
        cross = -jnp.einsum(
            "eij,ejk->eik", bottom, jnp.einsum("eij,ejk->eik", low, top, precision=FULL), precision=FULL
        )
        zero = jnp.zeros_like(cross).swapaxes(1, 2)
        return jnp.concatenate(
            [jnp.concatenate([top, zero], 2), jnp.concatenate([cross, bottom], 2)], 1
        )
    return pl.pallas_call(
        inverse_factor_kernel,
        out_shape=jax.ShapeDtypeStruct(gram.shape, jnp.float32),
        in_specs=[pl.BlockSpec(memory_space=pltpu.VMEM)],
        out_specs=pl.BlockSpec(memory_space=pltpu.VMEM),
        scratch_shapes=[pltpu.VMEM((matrices, size, size), jnp.float32)] * 2,
        cost_estimate=pl.CostEstimate(
            flops=size * size * size * 4 * matrices, bytes_accessed=8 * size * size * matrices, transcendentals=0
        ),
        name="inverse_factor",
    )(gram)


def swap(value, axis, mask):
    size = lax.axis_size(axis)
    return lax.ppermute(value, axis, [(i, i ^ mask) for i in range(size)])


def levels_of(size):
    return [(1, 0) if i == 0 else ((2 << i) - 2, i) for i in range(size.bit_length() - 1)]


def side_of(index, bit):
    if bit == 0:
        return index & 1
    return ((index >> bit) ^ (index >> (bit + 1))) & 1


def keep_half(value, axis, mask, side):
    half = value.shape[0] // 2
    own = lax.dynamic_slice_in_dim(value, side * half, half, 0)
    other = lax.dynamic_slice_in_dim(value, (1 - side) * half, half, 0)
    return own + swap(other, axis, mask)


def both_halves(value, axis, mask, side):
    other = swap(value, axis, mask)
    return jnp.where(
        side == 0, jnp.concatenate([value, other], 0), jnp.concatenate([other, value], 0)
    )


def sum_halving(value, axis, levels):
    index = lax.axis_index(axis)
    for mask, bit in levels:
        value = keep_half(value, axis, mask, side_of(index, bit))
    for mask, bit in reversed(levels):
        value = both_halves(value, axis, mask, side_of(index, bit))
    return value


def sum_doubling(value, axis, levels):
    for mask, _ in levels:
        value = value + swap(value, axis, mask)
    return value


def sum_near_first(value, axis, levels):
    index = lax.axis_index(axis)
    mask, bit = levels[0]
    side = side_of(index, bit)
    value = keep_half(value, axis, mask, side)
    value = sum_doubling(value, axis, levels[1:])
    return both_halves(value, axis, mask, side)


def general_body(momentum, gradient, q_factor):
    matrices, local_rows, local_cols = momentum.shape
    rank_width = q_factor.shape[2]
    total_rows = local_rows * lax.axis_size("fsdp")
    total_cols = local_cols * lax.axis_size("dp")
    dp_levels = levels_of(lax.axis_size("dp"))
    fsdp_levels = levels_of(lax.axis_size("fsdp"))
    buffers = [momentum[e] + gradient[e].astype(jnp.float32) for e in range(matrices)]
    lefts, grams, rights = [], [], []
    for e in range(matrices):
        partial_value = jnp.einsum("cn,nr->cr", buffers[e], q_factor[e], precision=THREE)
        order = dp_levels if e % 2 == 0 else dp_levels[1:2] + dp_levels[:1] + dp_levels[2:]
        left = sum_halving(partial_value, "dp", order)
        gram = jnp.einsum("cr,ck->rk", left, left, precision=FULL)
        lefts.append(left)
        grams.append(sum_doubling(gram, "fsdp", fsdp_levels))
        right_raw = jnp.einsum("cn,cr->nr", buffers[e], left, precision=THREE)
        rights.append(sum_near_first(right_raw, "fsdp", fsdp_levels))
    inverse = inverse_factor(jnp.stack(grams))
    orthos = [jnp.einsum("cr,kr->ck", lefts[e], inverse[e], precision=FULL) for e in range(matrices)]
    factors = [jnp.einsum("nr,kr->nk", rights[e], inverse[e], precision=FULL) for e in range(matrices)]
    squares = jnp.stack([jnp.sum(f * f, axis=0) for f in factors])
    squares = sum_doubling(squares, "dp", dp_levels)
    col_scale = lax.rsqrt(squares / total_cols + epsilon)
    rms = jnp.sqrt(jnp.float32(total_rows) / jnp.float32(rank_width))
    momenta, updates, new_qs = [], [], []
    for e in range(matrices):
        feedback = jnp.einsum("cr,nr->cn", orthos[e], factors[e], precision=ONE)
        momenta.append(buffers[e] - (1.0 - ema_decay) * feedback)
        new_q = factors[e] * col_scale[e][None, :]
        new_qs.append(new_q)
        direction = jnp.einsum("cr,nr->cn", orthos[e] * rms, new_q, precision=THREE)
        updates.append(direction.astype(jnp.bfloat16))
    return (jnp.stack(momenta), jnp.stack(updates), jnp.stack(new_qs))


def split(value):
    high = value.astype(BF16)
    return high, (value - high.astype(F32)).astype(BF16)


def dot(a, b):
    return jnp.dot(a, b, preferred_element_type=F32)


def dot_rows(a, b):
    return lax.dot_general(a, b, (((1,), (1,)), ((), ())), preferred_element_type=F32)


def eliminate(work, size):
    lanes = lax.broadcasted_iota(jnp.int32, (1, size), 1)
    rows = lax.broadcasted_iota(jnp.int32, (size, 1), 0)
    eight = lax.broadcasted_iota(jnp.int32, (8, 1), 0)

    def step(it, carry):
        base = pl.multiple_of(it * 8, 8)
        whole = work[...]
        block = work[pl.ds(base, 8), :]
        columns, pivots = [], []
        for j in range(8):
            here = lanes == base + j
            columns.append(jnp.sum(jnp.where(here, whole[:, :size], 0.0), axis=1, keepdims=True))
            pivots.append(jnp.sum(jnp.where(here, block[:, :size], 0.0), axis=1, keepdims=True))
        scaled, roots = [], []
        for k in range(8):
            root = lax.rsqrt(pivots[k][k : k + 1, :])
            inverse = root * root
            below = jnp.where(eight > k, pivots[k], 0.0)
            row = block[k : k + 1, :] * inverse
            block = block - below * row
            for j in range(k + 1, 8):
                factor = pivots[j][k : k + 1, :] * inverse
                pivots[j] = pivots[j] - below * factor
                columns[j] = columns[j] - columns[k] * factor
            scaled.append(row)
            roots.append(root)
        under = rows >= base + 8
        for k in range(8):
            whole = whole - jnp.where(under, columns[k], 0.0) * scaled[k]
        work[...] = whole
        root = roots[0]
        for k in range(1, 8):
            root = jnp.where(eight == k, roots[k], root)
        work[pl.ds(base, 8), :] = block * root
        return carry

    lax.fori_loop(0, size // 8, step, 0)


class Plan:
    def __init__(self, mesh, momentum, q_factor):
        self.matrices, self.rows, self.cols = momentum.shape
        self.rank = q_factor.shape[2]
        self.half_rank = self.rank // 2
        self.dp, self.fsdp = mesh.shape["dp"], mesh.shape["fsdp"]
        self.pairs = 4
        self.chunk = self.rows // (2 * self.pairs)
        self.half = self.chunk // 2
        self.width = 256
        self.tiles = self.cols // self.width

    def fits(self):
        return (
            self.dp == 8
            and self.fsdp == 4
            and self.rank == 256
            and self.rows % (32 * self.pairs) == 0
            and self.rows % 128 == 0
            and self.cols % (2 * self.width) == 0
            and self.rows % (16 * self.tiles) == 0
            and self.matrices * self.rows * self.cols <= 6 << 20
        )


def factor_kernel(
    plan,
    mom,
    grad,
    q,
    left_out,
    inverse_out,
    fact_out,
    square_out,
    bh,
    bl,
    mst,
    gst,
    qst,
    qh,
    ql,
    left,
    final,
    a_y,
    a_z1,
    a_z2,
    b_z1,
    b_z2,
    b_y,
    turned,
    turned_split,
    own,
    from_core,
    from_x,
    right,
    gram0,
    gram1,
    gram2,
    gram_core,
    gram_x,
    work,
    inverse,
    sq,
    sq_in,
    in_sem,
    q_sem,
    l_send,
    l_recv,
    r_send,
    r_recv,
    g_send,
    g_recv,
    s_send,
    s_recv,
    out_sem,
):
    E, K, H = plan.matrices, plan.rank, plan.half_rank
    NP, CH, HF, W, T = plan.pairs, plan.chunk, plan.half, plan.width, plan.tiles
    R = plan.rows
    d, f = lax.axis_index("dp"), lax.axis_index("fsdp")
    y, z = d % 2, d // 2
    core = f % 2
    mid = jnp.logical_or(z == 1, z == 2)
    leaf = jnp.logical_not(mid)
    zside = z // 2
    y_peer = (z * 2 + 1 - y, f)
    z_peer = ((z + 1 - 2 * (z % 2)) * 2 + y, f)
    m_peer = ((3 - z) * 2 + y, f)
    x_peer = (d, (f + 2) % 4)
    c_peer = (d, f + 1 - 2 * core)

    def remote(src, dst, send, recv, peer):
        return pltpu.make_async_remote_copy(
            src_ref=src, dst_ref=dst, send_sem=send, recv_sem=recv, device_id=peer, device_id_type=MESH
        )

    drains = []

    def start(copy, when=None):
        if when is None:
            copy.start()
        else:
            pl.when(when)(copy.start)
        drains.append((copy, when))

    def load(e, index, slot):
        at = pl.ds(pl.multiple_of(index * CH, CH), CH)
        return (
            pltpu.make_async_copy(mom.at[e, at, :], mst.at[slot], in_sem.at[0, slot]),
            pltpu.make_async_copy(grad.at[e, at, :], gst.at[slot], in_sem.at[1, slot]),
        )

    def load_q(e):
        return pltpu.make_async_copy(q.at[e], qst, q_sem)

    load_q(0).start()
    for slot in range(2):
        for copy in load(0, slot, slot):
            copy.start()

    barrier = pltpu.get_barrier_semaphore()
    for peer in (y_peer, z_peer, m_peer, x_peer, c_peer):
        pl.semaphore_signal(barrier, inc=1, device_id=peer, device_id_type=MESH)

    def left_products(e):
        load_q(e).wait()
        for c in range(0, plan.cols, 256):
            high, low = split(qst[c : c + 256, :])
            qh[c : c + 256, :] = high
            ql[c : c + 256, :] = low
        if e + 1 < E:
            load_q(e + 1).start()

        def pair(p, carry):
            for color in range(2):
                index = p * 2 + color
                at = pl.ds(pl.multiple_of(index * CH, CH), CH)
                for copy in load(e, index, color):
                    copy.wait()
                for c in range(0, plan.cols, 512):
                    cs = slice(c, c + 512)
                    high, low = split(mst[color, :, cs] + gst[color, :, cs].astype(F32))
                    bh[e, at, cs] = high
                    bl[e, at, cs] = low

                @pl.when(p < NP - 1)
                def _():
                    for copy in load(e, index + 2, color):
                        copy.start()

                if e + 1 < E:

                    @pl.when(p == NP - 1)
                    def _():
                        for copy in load(e + 1, color, color):
                            copy.start()

                b_high, b_low = bh[e, at, :], bl[e, at, :]
                total = dot(b_high, qh[...]) + dot(b_low, qh[...]) + dot(b_high, ql[...])
                left[e, 0, at, :] = total[:, :H]
                left[e, 1, at, :] = total[:, H:]
            return carry

        lax.fori_loop(0, NP, pair, 0)

    def rows_of(color, p, part=None):
        base = (2 * p + color) * CH
        if part is None:
            return pl.ds(base, CH)
        return pl.ds(pl.multiple_of(base + part * HF, HF), HF)

    def copies(e, h, p):
        u = (e * 2 + h) * NP + p
        s, r = (lambda i: l_send.at[u, i]), (lambda i: l_recv.at[u, i])
        part = lambda ref, color, which=None: ref.at[e, h, rows_of(color, p, which), :]
        mine, other = part(left, 0, y), part(left, 0, 1 - y)
        done, done_other = part(final, 0, y), part(final, 0, 1 - y)
        zmine, zother = part(left, 1, zside), part(left, 1, 1 - zside)
        zdone, zdone_other = part(final, 1, zside), part(final, 1, 1 - zside)
        return dict(
            a0=remote(other, a_y.at[u], s(0), r(0), y_peer),
            a1=remote(mine, a_z1.at[u], s(1), r(1), z_peer),
            a2=remote(mine, a_z2.at[u], s(1), r(2), m_peer),
            a3=remote(done, done, s(2), r(1), z_peer),
            a4=remote(done, done, s(3), r(3), y_peer),
            a5=remote(done_other, done_other, s(3), r(3), y_peer),
            b0=remote(part(left, 1), b_z1.at[u], s(4), r(4), z_peer),
            b1=remote(zother, b_z2.at[u], s(4), r(5), m_peer),
            b2=remote(zmine, b_y.at[u], s(5), r(6), y_peer),
            b3=remote(zdone, zdone, s(6), r(7), m_peer),
            b3w=remote(zdone_other, zdone_other, s(6), r(7), m_peer),
            b4=remote(zdone, zdone, s(7), r(4), z_peer),
            b5=remote(zdone_other, zdone_other, s(8), r(5), z_peer),
        ), (e, h, p, u)

    table = [copies(e, h, p) for e in range(E) for h in range(2) for p in range(NP)]

    def stage(k, s):
        c, (e, h, p, u) = table[k]
        at = lambda color, part=None: (e, h, rows_of(color, p, part), slice(None))
        if s == 0:
            start(c["a0"])
            start(c["b0"], leaf)
        elif s == 1:
            c["a0"].wait_recv()
            left[at(0, y)] = left[at(0, y)] + a_y[u]
            start(c["a1"], leaf)

            @pl.when(mid)
            def _():
                c["b0"].wait_recv()
                left[at(1)] = left[at(1)] + b_z1[u]

            start(c["b1"], mid)
        elif s == 2:

            @pl.when(mid)
            def _():
                c["a1"].wait_recv()
                left[at(0, y)] = left[at(0, y)] + a_z1[u]
                c["a2"].start()
                c["b1"].wait_recv()
                left[at(1, zside)] = left[at(1, zside)] + b_z2[u]
                c["b2"].start()

            drains.append((c["a2"], mid))
            drains.append((c["b2"], mid))
        elif s == 3:

            @pl.when(mid)
            def _():
                c["a2"].wait_recv()
                final[at(0, y)] = left[at(0, y)] + a_z2[u]
                c["a3"].start()
                c["a4"].start()
                c["b2"].wait_recv()
                final[at(1, zside)] = left[at(1, zside)] + b_y[u]
                c["b3"].start()
                c["b4"].start()

            for name in ("a3", "a4", "b3", "b4"):
                drains.append((c[name], mid))
        elif s == 4:

            @pl.when(leaf)
            def _():
                c["a3"].wait_recv()
                c["a4"].start()

            drains.append((c["a4"], leaf))

            @pl.when(mid)
            def _():
                c["b3w"].wait_recv()
                c["b5"].start()

            drains.append((c["b5"], mid))
        elif s == 5:
            c["a5"].wait_recv()

            @pl.when(leaf)
            def _():
                c["b4"].wait_recv()
                c["b5"].wait_recv()

    def write_left(e, h):
        return pltpu.make_async_copy(final.at[e, h], left_out.at[e, h], out_sem.at[e, h])

    def gram_part(ref, e, h):
        return ref.at[e, h, :, pl.ds(0, H * (h + 1))]

    def gram_copy(e, h, which):
        u = e * 2 + h
        src, dst = ((gram0, gram_core), (gram1, gram_x))[which]
        peer = (c_peer, x_peer)[which]
        return remote(gram_part(src, e, h), gram_part(dst, e, h), g_send.at[u, which], g_recv.at[u, which], peer)

    def gram_first(e, h):
        write_left(e, h).start()
        for c in range(0, R, 128):
            turned[:, c : c + 128] = final[e, h, c : c + 128, :].T
        for j in range(h + 1):
            gram0[e, h, :, j * H : (j + 1) * H] = jnp.dot(
                turned[...], final[e, j], precision=FULL, preferred_element_type=F32
            )
        start(gram_copy(e, h, 0))
        high, low = split(turned[...])
        turned_split[:H, :] = high
        turned_split[H:, :] = low

    def gram_second(e, h):
        gram_copy(e, h, 0).wait_recv()
        w = slice(0, H * (h + 1))
        gram1[e, h, :, w] = gram0[e, h, :, w] + gram_core[e, h, :, w]
        start(gram_copy(e, h, 1))

    def gram_third(e, h):
        gram_copy(e, h, 1).wait_recv()
        w = slice(0, H * (h + 1))
        gram2[e, h, :, w] = gram1[e, h, :, w] + gram_x[e, h, :, w]

    def full(a, b, rows=False):
        if rows:
            return lax.dot_general(
                a, b, (((1,), (1,)), ((), ())), precision=FULL, preferred_element_type=F32
            )
        return jnp.dot(a, b, precision=FULL, preferred_element_type=F32)

    def factorize(e, h):
        eye = jnp.where(
            lax.broadcasted_iota(jnp.int32, (H, H), 0) == lax.broadcasted_iota(jnp.int32, (H, H), 1), 1.0, 0.0
        ).astype(F32)
        if h == 0:
            work[:, :H] = gram2[e, 0, :, :H]
            work[:, H:] = eye
            eliminate(work, H)
            inverse[e, :H, :H] = work[:, H:]
            inverse[e, :H, H:] = jnp.zeros((H, H), F32)
        else:
            top = inverse[e, :H, :H]
            low = full(gram2[e, 1, :, :H], top, rows=True)
            work[:, :H] = gram2[e, 1, :, H:] - full(low, low, rows=True)
            work[:, H:] = eye
            cross = full(low, top)
            eliminate(work, H)
            bottom = work[:, H:]
            inverse[e, H:, H:] = bottom
            inverse[e, H:, :H] = -full(bottom, cross)

    def right_copy(e, h, s, which):
        u = e * 2 + h
        tile, other = 2 * s + core, 2 * s + 1 - core
        hs = pl.ds(h * H, H)
        if which == 0:
            src, dst, peer = own.at[u, other], from_core.at[u, s], c_peer
        elif which == 1:
            src, dst, peer = own.at[u, tile], from_x.at[u, s], x_peer
        else:
            tile = tile if which == 2 else other
            src = dst = right.at[e, tile, hs, :]
            peer, which = c_peer, 2
        return remote(src, dst, r_send.at[u, s, which], r_recv.at[u, s, which], peer)

    def right_products(e, h):
        u = e * 2 + h

        def product(tile):
            at = pl.ds(pl.multiple_of(tile * W, W), W)
            both = dot(turned_split[...], bh[e, :, at])
            own[u, tile] = both[:H] + both[H:] + dot(turned_split[:H, :], bl[e, :, at])

        def forward(s):
            right_copy(e, h, s, 0).wait_recv()
            tile = 2 * s + core
            own[u, tile] = own[u, tile] + from_core[u, s]
            right_copy(e, h, s, 1).start()

        def step(s, carry):
            product(2 * s + 1 - core)
            right_copy(e, h, s, 0).start()
            product(2 * s + core)
            pl.when(s > 0)(lambda: forward(s - 1))
            return carry

        lax.fori_loop(0, T // 2, step, 0)
        forward(T // 2 - 1)
        for s in range(T // 2):
            drains.append((right_copy(e, h, s, 0), None))
            drains.append((right_copy(e, h, s, 1), None))

    def right_sums(e, h):
        u = e * 2 + h
        for s in range(T // 2):
            right_copy(e, h, s, 1).wait_recv()
            tile = 2 * s + core
            right[e, tile, pl.ds(h * H, H), :] = own[u, tile] + from_x[u, s]
            right_copy(e, h, s, 2).start()

    def right_others(e, h):
        for s in range(T // 2):
            right_copy(e, h, s, 3).wait_recv()

    def write_fact(e, j):
        return pltpu.make_async_copy(right.at[e, j], fact_out.at[e, j], out_sem.at[e, 2 + j])

    def write_inverse(e):
        return pltpu.make_async_copy(inverse.at[e], inverse_out.at[e], out_sem.at[e, 2 + T])

    def write_square(e):
        return pltpu.make_async_copy(sq.at[e, 3], square_out.at[e], out_sem.at[e, 3 + T])

    def square_copy(e, r):
        peer = (y_peer, z_peer, m_peer)[r]
        return remote(sq.at[e, r], sq_in.at[e, r], s_send.at[e, r], s_recv.at[e, r], peer)

    def factors(e):
        write_inverse(e).start()
        for s in range(T // 2):
            right_copy(e, 0, s, 2).wait_send()
            right_copy(e, 1, s, 2).wait_send()
        x_high, x_low = split(inverse[e])
        total = jnp.zeros((K, 128), F32)
        for j in range(T):
            high, low = split(right[e, j])
            value = dot(x_high, high) + dot(x_low, high) + dot(x_high, low)
            right[e, j] = value
            write_fact(e, j).start()
            for c in range(0, W, 128):
                total = total + value[:, c : c + 128] * value[:, c : c + 128]
        row = jnp.sum(total.T, axis=0, keepdims=True)
        sq[e, 0] = jnp.broadcast_to(row, (8, K))
        start(square_copy(e, 0))

    def square_round(e, r):
        square_copy(e, r).wait_recv()
        sq[e, r + 1] = sq[e, r] + sq_in[e, r]
        if r < 2:
            start(square_copy(e, r + 1))
        else:
            write_square(e).start()

    left_products(0)
    pl.semaphore_wait(barrier, 5)
    SLOTS, STAGES = len(table), 6
    after = {}
    def add(t, *jobs):
        after.setdefault(t, []).extend(jobs)

    add(1, lambda: left_products(1))
    order = [(e, h) for e in range(E) for h in range(2)]
    for u, (e, h) in enumerate(order):
        t = (u + 1) * NP - 1 + STAGES - 1
        add(t, functools.partial(gram_first, e, h), functools.partial(gram_second, e, h), functools.partial(right_products, e, h))
        add(t + 1, functools.partial(gram_third, e, h))
        add(t + 2, functools.partial(factorize, e, h))
        add(t + 3, functools.partial(right_sums, e, h))
        if h == 1:
            add(t + 4, functools.partial(right_others, e, 0), functools.partial(right_others, e, 1), functools.partial(factors, e))
            for r in range(3):
                add(t + 5 + r, functools.partial(square_round, e, r))
    last = max(after)
    for t in range(max(last + 1, SLOTS + STAGES)):
        for s in reversed(range(STAGES)):
            if 0 <= t - s < SLOTS:
                stage(t - s, s)
        for job in after.get(t, []):
            job()

    for copy, when in drains:
        if when is None:
            copy.wait_send()
        else:
            pl.when(when)(copy.wait_send)
    for e in range(E):
        for h in range(2):
            write_left(e, h).wait()
        for j in range(T):
            write_fact(e, j).wait()
        write_inverse(e).wait()
        write_square(e).wait()


def factor_call(plan, momentum, gradient, q_factor):
    E, R, C, K, H = plan.matrices, plan.rows, plan.cols, plan.rank, plan.half_rank
    NP, CH, HF, W, T = plan.pairs, plan.chunk, plan.half, plan.width, plan.tiles
    U = E * 2 * NP
    any_spec = pl.BlockSpec(memory_space=pl.ANY)
    vmem = pltpu.VMEM
    flops = 14 * E * R * C * K
    return pl.pallas_call(
        functools.partial(factor_kernel, plan),
        out_shape=(
            jax.ShapeDtypeStruct((E, 2, R, H), F32),
            jax.ShapeDtypeStruct((E, K, K), F32),
            jax.ShapeDtypeStruct((E, T, K, W), F32),
            jax.ShapeDtypeStruct((E, 8, K), F32),
        ),
        in_specs=[any_spec] * 3,
        out_specs=(any_spec,) * 4,
        scratch_shapes=[
            vmem((E, R, C), BF16),
            vmem((E, R, C), BF16),
            vmem((2, CH, C), F32),
            vmem((2, CH, C), BF16),
            vmem((C, K), F32),
            vmem((C, K), BF16),
            vmem((C, K), BF16),
            vmem((E, 2, R, H), F32),
            vmem((E, 2, R, H), F32),
            vmem((U, HF, H), F32),
            vmem((U, HF, H), F32),
            vmem((U, HF, H), F32),
            vmem((U, CH, H), F32),
            vmem((U, HF, H), F32),
            vmem((U, HF, H), F32),
            vmem((H, R), F32),
            vmem((K, R), BF16),
            vmem((E * 2, T, H, W), F32),
            vmem((E * 2, T // 2, H, W), F32),
            vmem((E * 2, T // 2, H, W), F32),
            vmem((E, T, K, W), F32),
            vmem((E, 2, H, K), F32),
            vmem((E, 2, H, K), F32),
            vmem((E, 2, H, K), F32),
            vmem((E, 2, H, K), F32),
            vmem((E, 2, H, K), F32),
            vmem((H, K), F32),
            vmem((E, K, K), F32),
            vmem((E, 4, 8, K), F32),
            vmem((E, 3, 8, K), F32),
            pltpu.SemaphoreType.DMA((2, 2)),
            pltpu.SemaphoreType.DMA,
            pltpu.SemaphoreType.DMA((U, 9)),
            pltpu.SemaphoreType.DMA((U, 8)),
            pltpu.SemaphoreType.DMA((E * 2, T // 2, 3)),
            pltpu.SemaphoreType.DMA((E * 2, T // 2, 3)),
            pltpu.SemaphoreType.DMA((E * 2, 2)),
            pltpu.SemaphoreType.DMA((E * 2, 2)),
            pltpu.SemaphoreType.DMA((E, 3)),
            pltpu.SemaphoreType.DMA((E, 3)),
            pltpu.SemaphoreType.DMA((E, T + 4)),
        ],
        compiler_params=pltpu.CompilerParams(
            collective_id=0, has_side_effects=True, vmem_limit_bytes=67043328
        ),
        cost_estimate=pl.CostEstimate(flops=flops, bytes_accessed=6 * E * R * C, transcendentals=0),
        name="dion_factors",
    )(momentum, gradient, q_factor)


def output_kernel(
    rms, total_cols, mom, grad, left, inverse, fact, square, new_mom, update, new_q, fh, fl, xh, xl
):
    tiles, width = fact.shape[1], fact.shape[3]
    step = pl.program_id(1)

    @pl.when(step == 0)
    def _():
        for j in range(tiles):
            high, low = split(fact[0, j])
            fh[j] = high
            fl[j] = low
        high, low = split(inverse[0])
        xh[...] = high
        xl[...] = low

    scale = lax.rsqrt(square[0, 0:1, :] / total_cols + epsilon)
    high, low = split(jnp.concatenate([left[0, 0], left[0, 1]], axis=1))
    ortho = dot_rows(high, xh[...]) + dot_rows(low, xh[...]) + dot_rows(high, xl[...])
    feed = (ortho * (1.0 - ema_decay)).astype(BF16)
    high, low = split(ortho * (scale * rms))
    rows = high.shape[0]
    stack = jnp.concatenate([feed, high, low], axis=0)
    for j in range(tiles):
        at = slice(j * width, (j + 1) * width)
        value = dot(stack, fh[j])
        direction = value[rows : 2 * rows] + value[2 * rows :] + dot(high, fl[j])
        new_mom[0, :, at] = (mom[0, :, at] + grad[0, :, at].astype(F32)) - value[:rows]
        update[0, :, at] = direction.astype(BF16)
    new_q[0] = fact[0, step].T * scale


def output_call(plan, momentum, gradient, left, inverse, fact, square):
    E, R, C, K, H = plan.matrices, plan.rows, plan.cols, plan.rank, plan.half_rank
    T, W = plan.tiles, plan.width
    block = R // T
    rms = math.sqrt(R * plan.fsdp / K)
    tall = pl.BlockSpec((1, block, C), lambda e, i: (e, i, 0))
    return pl.pallas_call(
        functools.partial(output_kernel, rms, float(C * plan.dp)),
        grid=(E, T),
        out_shape=(
            jax.ShapeDtypeStruct((E, R, C), F32),
            jax.ShapeDtypeStruct((E, R, C), BF16),
            jax.ShapeDtypeStruct((E, C, K), F32),
        ),
        in_specs=[
            tall,
            tall,
            pl.BlockSpec((1, 2, block, H), lambda e, i: (e, 0, i, 0)),
            pl.BlockSpec((1, K, K), lambda e, i: (e, 0, 0)),
            pl.BlockSpec((1, T, K, W), lambda e, i: (e, 0, 0, 0)),
            pl.BlockSpec((1, 8, K), lambda e, i: (e, 0, 0)),
        ],
        out_specs=(tall, tall, pl.BlockSpec((1, W, K), lambda e, i: (e, i, 0))),
        scratch_shapes=[
            pltpu.VMEM((T, K, W), BF16),
            pltpu.VMEM((T, K, W), BF16),
            pltpu.VMEM((K, K), BF16),
            pltpu.VMEM((K, K), BF16),
        ],
        compiler_params=pltpu.CompilerParams(vmem_limit_bytes=48 << 20),
        cost_estimate=pl.CostEstimate(
            flops=8 * E * R * C * K, bytes_accessed=12 * E * R * C, transcendentals=0
        ),
        name="dion_outputs",
    )(momentum, gradient, left, inverse, fact, square)


def body(mesh, momentum, gradient, q_factor):
    plan = Plan(mesh, momentum, q_factor)
    if not plan.fits():
        return general_body(momentum, gradient, q_factor)
    left, inverse, fact, square = factor_call(plan, momentum, gradient, q_factor)
    return output_call(plan, momentum, gradient, left, inverse, fact, square)


def solution(mesh):
    placed = (P(None, "fsdp", "dp"), P(None, "fsdp", "dp"), P(None, "dp", None))
    return jax.shard_map(
        functools.partial(body, mesh),
        mesh=mesh,
        in_specs=placed,
        out_specs=(P(None, "fsdp", "dp"), P(None, "fsdp", "dp"), P(None, "dp", None)),
        check_vma=False,
    )
```

profile of v0, /device:TPU:12, one launch (start us, length us, event | category | flops | bytes accessed | tf_op | source)
XLA Modules:
  0.0 206.8 jit_solution(18348274104516236461)
XLA Ops:
  0.6 164.6 %dion_factors.1 = (f32[2,2,1536,128]{3,2,1,0:T(8,128)}, f32[2,256,256]{2,1,0:T(8,128)}, f32[2,8,256,256]{3,2,1,0:T(8,128)}, f32[2,8,256]{2,1,0:T(8,128)}) custom-call(f32[2,1536,2048]{2,1,0:T(8,128)} %mom.3, bf16[2,1536,2048]{2,1,0:T(8,128)(2,1)} %grad.3, f32[2,2048,256]{2,1,0:T(8,128)} %q.1), custom_call_target="tpu_custom_call" | custom-call | flops 22548578304 | bytes 37748736 | tf_op jit(solution)/shard_map/dion_factors/pallas_call | solution.py:692
  165.2 0.0 copy-start
  165.2 1.9 copy-done
  167.1 0.0 copy-start.1
  167.1 1.0 copy-done.1
  168.1 0.0 copy-start.2
  168.1 0.7 copy-done.2
  168.9 37.9 %dion_outputs.1 = (f32[2,1536,2048]{2,1,0:T(8,128)}, bf16[2,1536,2048]{2,1,0:T(8,128)(2,1)}, f32[2,2048,256]{2,1,0:T(8,128)}) custom-call(f32[2,1536,2048]{2,1,0:T(8,128)} %mom.3, bf16[2,1536,2048]{2,1,0:T(8,128)(2,1)} %grad.3, f32[2,2,1536,128]{3,2,1,0:T(8,128)S(1)} %copy-done, f32[2,256,256]{2,1,0:T(8,128)S(1)} %copy-done.1, ...), custom_call_target="tpu_custom_call" | custom-call | flops 12884901888 | bytes 75497472 | tf_op jit(solution)/shard_map/dion_outputs/pallas_call | solution.py:791
Async XLA Ops:
  165.2 1.9 copy-start
  167.1 1.0 copy-start.1
  168.1 0.7 copy-start.2
where the time goes:
time: 207 us
  Pallas kernels  202 us (98%)
  local copies, waits for them, and re-layouts  3.64 us (2%)
    pallas_call x1, Pallas kernels, factor_call(): pl.pallas_call(functools.partial(factor_kernel, plan), out_shape=(jax.Sha...  165 us
    pallas_call x1, Pallas kernels, output_call(): pl.pallas_call(functools.partial(output_kernel, rms, float(C * plan.dp)),...  37.9 us

commit v1 on v0

v1 whole, which is shorter than its diff:
```python
import functools
import math

import jax
import jax.numpy as jnp
from jax import lax
from jax.experimental import pallas as pl
from jax.experimental.pallas import tpu as pltpu
from jax.sharding import PartitionSpec as P

MESH = pl.DeviceIdType.MESH
F32 = jnp.float32
BF16 = jnp.bfloat16

ema_decay = 0.75
epsilon = 1e-06
BLOCK = 128
FULL = lax.Precision.HIGHEST
THREE = lax.Precision.HIGH
ONE = lax.Precision.DEFAULT


def inverse_factor_kernel(gram_ref, out_ref, work_left, work_right):
    matrices, size, _ = gram_ref.shape
    rows = lax.broadcasted_iota(jnp.int32, (size, 1), 0)
    lanes = lax.broadcasted_iota(jnp.int32, (1, size), 1)
    eye = jnp.where(rows == lanes, 1.0, 0.0).astype(jnp.float32)
    for e in range(matrices):
        work_left[e] = gram_ref[e]
        work_right[e] = eye

    def step(k, carry):
        for e in range(matrices):
            left = work_left[e]
            right = work_right[e]
            row_left = work_left[e, pl.ds(k, 1), :]
            row_right = work_right[e, pl.ds(k, 1), :]
            pivot = jnp.sum(jnp.where(lanes == k, row_left, 0.0), axis=1, keepdims=True)
            inverse = lax.rsqrt(pivot)
            row_left = row_left * inverse
            row_right = row_right * inverse
            column = jnp.sum(jnp.where(lanes == k, left, 0.0), axis=1, keepdims=True)
            column = jnp.where(rows > k, column * inverse, 0.0)
            work_left[e] = left - column * row_left
            work_right[e] = jnp.where(rows == k, row_right, right - column * row_right)
        return carry

    lax.fori_loop(0, size, step, 0)
    for e in range(matrices):
        out_ref[e] = work_right[e]


def inverse_factor(gram):
    matrices, size, _ = gram.shape
    if size > BLOCK:
        half = size // 2
        top = inverse_factor(gram[:, :half, :half])
        low = jnp.einsum("eij,ekj->eik", gram[:, half:, :half], top, precision=FULL)
        rest = gram[:, half:, half:] - jnp.einsum("eij,ekj->eik", low, low, precision=FULL)
        bottom = inverse_factor(rest)
        cross = -jnp.einsum(
            "eij,ejk->eik", bottom, jnp.einsum("eij,ejk->eik", low, top, precision=FULL), precision=FULL
        )
        zero = jnp.zeros_like(cross).swapaxes(1, 2)
        return jnp.concatenate(
            [jnp.concatenate([top, zero], 2), jnp.concatenate([cross, bottom], 2)], 1
        )
    return pl.pallas_call(
        inverse_factor_kernel,
        out_shape=jax.ShapeDtypeStruct(gram.shape, jnp.float32),
        in_specs=[pl.BlockSpec(memory_space=pltpu.VMEM)],
        out_specs=pl.BlockSpec(memory_space=pltpu.VMEM),
        scratch_shapes=[pltpu.VMEM((matrices, size, size), jnp.float32)] * 2,
        cost_estimate=pl.CostEstimate(
            flops=size * size * size * 4 * matrices, bytes_accessed=8 * size * size * matrices, transcendentals=0
        ),
        name="inverse_factor",
    )(gram)


def swap(value, axis, mask):
    size = lax.axis_size(axis)
    return lax.ppermute(value, axis, [(i, i ^ mask) for i in range(size)])


def levels_of(size):
    return [(1, 0) if i == 0 else ((2 << i) - 2, i) for i in range(size.bit_length() - 1)]


def side_of(index, bit):
    if bit == 0:
        return index & 1
    return ((index >> bit) ^ (index >> (bit + 1))) & 1


def keep_half(value, axis, mask, side):
    half = value.shape[0] // 2
    own = lax.dynamic_slice_in_dim(value, side * half, half, 0)
    other = lax.dynamic_slice_in_dim(value, (1 - side) * half, half, 0)
    return own + swap(other, axis, mask)


def both_halves(value, axis, mask, side):
    other = swap(value, axis, mask)
    return jnp.where(
        side == 0, jnp.concatenate([value, other], 0), jnp.concatenate([other, value], 0)
    )


def sum_halving(value, axis, levels):
    index = lax.axis_index(axis)
    for mask, bit in levels:
        value = keep_half(value, axis, mask, side_of(index, bit))
    for mask, bit in reversed(levels):
        value = both_halves(value, axis, mask, side_of(index, bit))
    return value


def sum_doubling(value, axis, levels):
    for mask, _ in levels:
        value = value + swap(value, axis, mask)
    return value


def sum_near_first(value, axis, levels):
    index = lax.axis_index(axis)
    mask, bit = levels[0]
    side = side_of(index, bit)
    value = keep_half(value, axis, mask, side)
    value = sum_doubling(value, axis, levels[1:])
    return both_halves(value, axis, mask, side)


def general_body(momentum, gradient, q_factor):
    matrices, local_rows, local_cols = momentum.shape
    rank_width = q_factor.shape[2]
    total_rows = local_rows * lax.axis_size("fsdp")
    total_cols = local_cols * lax.axis_size("dp")
    dp_levels = levels_of(lax.axis_size("dp"))
    fsdp_levels = levels_of(lax.axis_size("fsdp"))
    buffers = [momentum[e] + gradient[e].astype(jnp.float32) for e in range(matrices)]
    lefts, grams, rights = [], [], []
    for e in range(matrices):
        partial_value = jnp.einsum("cn,nr->cr", buffers[e], q_factor[e], precision=THREE)
        order = dp_levels if e % 2 == 0 else dp_levels[1:2] + dp_levels[:1] + dp_levels[2:]
        left = sum_halving(partial_value, "dp", order)
        gram = jnp.einsum("cr,ck->rk", left, left, precision=FULL)
        lefts.append(left)
        grams.append(sum_doubling(gram, "fsdp", fsdp_levels))
        right_raw = jnp.einsum("cn,cr->nr", buffers[e], left, precision=THREE)
        rights.append(sum_near_first(right_raw, "fsdp", fsdp_levels))
    inverse = inverse_factor(jnp.stack(grams))
    orthos = [jnp.einsum("cr,kr->ck", lefts[e], inverse[e], precision=FULL) for e in range(matrices)]
    factors = [jnp.einsum("nr,kr->nk", rights[e], inverse[e], precision=FULL) for e in range(matrices)]
    squares = jnp.stack([jnp.sum(f * f, axis=0) for f in factors])
    squares = sum_doubling(squares, "dp", dp_levels)
    col_scale = lax.rsqrt(squares / total_cols + epsilon)
    rms = jnp.sqrt(jnp.float32(total_rows) / jnp.float32(rank_width))
    momenta, updates, new_qs = [], [], []
    for e in range(matrices):
        feedback = jnp.einsum("cr,nr->cn", orthos[e], factors[e], precision=ONE)
        momenta.append(buffers[e] - (1.0 - ema_decay) * feedback)
        new_q = factors[e] * col_scale[e][None, :]
        new_qs.append(new_q)
        direction = jnp.einsum("cr,nr->cn", orthos[e] * rms, new_q, precision=THREE)
        updates.append(direction.astype(jnp.bfloat16))
    return (jnp.stack(momenta), jnp.stack(updates), jnp.stack(new_qs))


def split(value):
    high = value.astype(BF16)
    return high, (value - high.astype(F32)).astype(BF16)


def dot(a, b):
    return jnp.dot(a, b, preferred_element_type=F32)


def dot_rows(a, b):
    return lax.dot_general(a, b, (((1,), (1,)), ((), ())), preferred_element_type=F32)


def eliminate(work, size, part):
    top = part * (size // 2)
    lanes = lax.broadcasted_iota(jnp.int32, (1, size), 1)
    rows = lax.broadcasted_iota(jnp.int32, (size - top, 1), 0) + top
    eight = lax.broadcasted_iota(jnp.int32, (8, 1), 0)

    def step(it, carry):
        base = pl.multiple_of(it * 8, 8)
        whole = work[top:, :]
        block = work[pl.ds(base, 8), :]
        columns, pivots = [], []
        for j in range(8):
            here = lanes == base + j
            columns.append(jnp.sum(jnp.where(here, whole[:, :size], 0.0), axis=1, keepdims=True))
            pivots.append(jnp.sum(jnp.where(here, block[:, :size], 0.0), axis=1, keepdims=True))
        scaled, roots = [], []
        for k in range(8):
            root = lax.rsqrt(pivots[k][k : k + 1, :])
            inverse = root * root
            below = jnp.where(eight > k, pivots[k], 0.0)
            row = block[k : k + 1, :] * inverse
            block = block - below * row
            for j in range(k + 1, 8):
                factor = pivots[j][k : k + 1, :] * inverse
                pivots[j] = pivots[j] - below * factor
                columns[j] = columns[j] - columns[k] * factor
            scaled.append(row)
            roots.append(root)
        under = rows >= base + 8
        for k in range(8):
            whole = whole - jnp.where(under, columns[k], 0.0) * scaled[k]
        work[top:, :] = whole
        root = roots[0]
        for k in range(1, 8):
            root = jnp.where(eight == k, roots[k], root)
        work[pl.ds(base, 8), :] = block * root
        return carry

    lax.fori_loop(top // 8, (top + size // 2) // 8, step, 0)


class Plan:
    def __init__(self, mesh, momentum, q_factor):
        self.matrices, self.rows, self.cols = momentum.shape
        self.rank = q_factor.shape[2]
        self.half_rank = self.rank // 2
        self.dp, self.fsdp = mesh.shape["dp"], mesh.shape["fsdp"]
        self.pairs = 4
        self.chunk = self.rows // (2 * self.pairs)
        self.half = self.chunk // 2
        self.width = 256
        self.tiles = self.cols // self.width

    def fits(self):
        return (
            self.dp == 8
            and self.fsdp == 4
            and self.rank == 256
            and self.rows % (32 * self.pairs) == 0
            and self.rows % 128 == 0
            and self.cols % (4 * self.width) == 0
            and self.rows % (16 * self.tiles) == 0
            and self.matrices * self.rows * self.cols <= 6 << 20
        )


def factor_kernel(
    plan,
    mom,
    grad,
    q,
    left_out,
    inverse_out,
    fact_out,
    square_out,
    bh,
    bl,
    mst,
    gst,
    qh,
    ql,
    left,
    final,
    a_y,
    a_z1,
    a_z2,
    b_z1,
    b_z2,
    b_y,
    turned,
    turned_split,
    own,
    from_core,
    from_x,
    right,
    gram0,
    gram_core,
    gram_x,
    work,
    inverse,
    sq,
    sq_in,
    sq_all,
    in_sem,
    q_sem,
    l_send,
    l_recv,
    r_send,
    r_recv,
    g_send,
    g_recv,
    s_send,
    s_recv,
    out_sem,
):
    E, K, H = plan.matrices, plan.rank, plan.half_rank
    NP, CH, HF, W, T = plan.pairs, plan.chunk, plan.half, plan.width, plan.tiles
    R = plan.rows
    d, f = lax.axis_index("dp"), lax.axis_index("fsdp")
    y, z = d % 2, d // 2
    core = f % 2
    mid = jnp.logical_or(z == 1, z == 2)
    leaf = jnp.logical_not(mid)
    zside = z // 2
    y_peer = (z * 2 + 1 - y, f)
    z_peer = ((z + 1 - 2 * (z % 2)) * 2 + y, f)
    m_peer = ((3 - z) * 2 + y, f)
    x_peer = (d, (f + 2) % 4)
    c_peer = (d, f + 1 - 2 * core)

    def remote(src, dst, send, recv, peer):
        return pltpu.make_async_remote_copy(
            src_ref=src, dst_ref=dst, send_sem=send, recv_sem=recv, device_id=peer, device_id_type=MESH
        )

    PR, CS = 2 * CH, plan.cols // 2

    def load(n, side):
        e, at = n // NP, pl.ds(pl.multiple_of(lax.rem(n, NP) * PR, PR), PR)
        cs = pl.ds(side * CS, CS)
        return (
            pltpu.make_async_copy(mom.at[e, at, cs], mst.at[side], in_sem.at[0, side]),
            pltpu.make_async_copy(grad.at[e, at, cs], gst.at[side], in_sem.at[1, side]),
        )

    def load_q(e):
        return [
            pltpu.make_async_copy(q.at[e, pl.ds(j * W, W), :], right.at[E - 1, j], q_sem.at[j]) for j in range(T)
        ]

    for copy in load_q(0):
        copy.start()
    for slot in range(2):
        for copy in load(0, slot):
            copy.start()

    barrier = pltpu.get_barrier_semaphore()
    others = [(lax.rem(d + i, plan.dp), f) for i in range(1, plan.dp)]
    for peer in (*others, x_peer, c_peer):
        pl.semaphore_signal(barrier, inc=1, device_id=peer, device_id_type=MESH)

    def left_pair(n):
        e, p = n // NP, lax.rem(n, NP)

        @pl.when(p == 0)
        def _():
            for j, copy in enumerate(load_q(e)):
                copy.wait()
                high, low = split(right[E - 1, j])
                qh[j * W : (j + 1) * W, :] = high
                ql[j * W : (j + 1) * W, :] = low

            @pl.when(e + 1 < E)
            def _():
                for copy in load_q(e + 1):
                    copy.start()

        at = pl.ds(pl.multiple_of(p * PR, PR), PR)
        for side in range(2):
            for copy in load(n, side):
                copy.wait()
            total = jnp.zeros((PR, K), F32)
            for c in range(0, CS, 256):
                cs, ks = slice(c, c + 256), slice(side * CS + c, side * CS + c + 256)
                high, low = split(mst[side, :, cs] + gst[side, :, cs].astype(F32))
                bh[e, at, ks] = high
                bl[e, at, ks] = low
                both = dot(jnp.concatenate([high, low], axis=0), qh[ks, :])
                total = total + (both[:PR] + both[PR:] + dot(high, ql[ks, :]))

            @pl.when(n + 1 < E * NP)
            def _():
                for copy in load(n + 1, side):
                    copy.start()

            for h in range(2):
                part = total[:, h * H : (h + 1) * H]
                left[e * 2 + h, at, :] = part if side == 0 else left[e * 2 + h, at, :] + part

    def rows_of(color, p, part=None):
        base = (2 * p + color) * CH
        if part is None:
            return pl.ds(pl.multiple_of(base, CH), CH)
        return pl.ds(pl.multiple_of(base + part * HF, HF), HF)

    def copies(k):
        unit, p = k // NP, lax.rem(k, NP)
        s, r = (lambda i: l_send.at[k, i]), (lambda i: l_recv.at[k, i])
        part = lambda ref, color, which=None: ref.at[unit, rows_of(color, p, which), :]
        mine, other = part(left, 0, y), part(left, 0, 1 - y)
        done, done_other = part(final, 0, y), part(final, 0, 1 - y)
        zmine, zother = part(left, 1, zside), part(left, 1, 1 - zside)
        zdone, zdone_other = part(final, 1, zside), part(final, 1, 1 - zside)
        made = dict(
            a0=(other, a_y.at[k], s(0), r(0), y_peer),
            a1=(mine, a_z1.at[k], s(1), r(1), z_peer),
            a2=(mine, a_z2.at[k], s(1), r(2), m_peer),
            a3=(done, done, s(2), r(1), z_peer),
            a4=(done, done, s(3), r(3), y_peer),
            a5=(done_other, done_other, s(3), r(3), y_peer),
            b0=(part(left, 1), b_z1.at[k], s(4), r(4), z_peer),
            b1=(zother, b_z2.at[k], s(4), r(5), m_peer),
            b2=(zmine, b_y.at[k], s(5), r(6), y_peer),
            b3=(zdone, zdone, s(6), r(7), m_peer),
            b3w=(zdone_other, zdone_other, s(6), r(7), m_peer),
            b4=(zdone, zdone, s(7), r(4), z_peer),
            b5=(zdone_other, zdone_other, s(8), r(5), z_peer),
        )
        return lambda name: remote(*made[name])

    def stage(k, s):
        unit, p = k // NP, lax.rem(k, NP)
        c = copies(k)
        at = lambda color, part=None: (unit, rows_of(color, p, part), slice(None))
        if s == 0:
            c("a0").start()
            pl.when(leaf)(c("b0").start)
        elif s == 1:
            c("a0").wait_recv()
            left[at(0, y)] = left[at(0, y)] + a_y[k]

            @pl.when(leaf)
            def _():
                c("a1").start()

            @pl.when(mid)
            def _():
                c("b0").wait_recv()
                left[at(1)] = left[at(1)] + b_z1[k]
                c("b1").start()
        elif s == 2:

            @pl.when(mid)
            def _():
                c("a1").wait_recv()
                left[at(0, y)] = left[at(0, y)] + a_z1[k]
                c("a2").start()
                c("b1").wait_recv()
                left[at(1, zside)] = left[at(1, zside)] + b_z2[k]
                c("b2").start()
        elif s == 3:

            @pl.when(mid)
            def _():
                c("a2").wait_recv()
                final[at(0, y)] = left[at(0, y)] + a_z2[k]
                c("a3").start()
                c("a4").start()
                c("b2").wait_recv()
                final[at(1, zside)] = left[at(1, zside)] + b_y[k]
                c("b3").start()
                c("b4").start()
        elif s == 4:

            @pl.when(leaf)
            def _():
                c("a3").wait_recv()
                c("a4").start()

            @pl.when(mid)
            def _():
                c("b3w").wait_recv()
                c("b5").start()
        elif s == 5:
            c("a5").wait_recv()

            @pl.when(leaf)
            def _():
                c("b4").wait_recv()
                c("b5").wait_recv()

    SLOTS, STAGES, DELAYS = E * 2 * NP, 6, (0, 2, 3, 4, 5, 6)

    def slot(t):
        for s in reversed(range(STAGES)):
            k = t - DELAYS[s]
            pl.when(jnp.logical_and(k >= 0, k < SLOTS))(functools.partial(stage, k, s))

    def drain(k):
        c = copies(k)
        c("a0").wait_send()
        c("a4").wait_send()

        @pl.when(leaf)
        def _():
            c("b0").wait_send()
            c("a1").wait_send()

        @pl.when(mid)
        def _():
            for name in ("b1", "a2", "b2", "a3", "b3", "b4", "b5"):
                c(name).wait_send()

    def write_left(u):
        return pltpu.make_async_copy(final.at[u], left_out.at[u // 2, lax.rem(u, 2)], out_sem.at[u // 2, lax.rem(u, 2)])

    def gram_copy(u, which):
        src, dst = ((gram0, gram_core), (gram_core, gram_x))[which]
        peer = (c_peer, x_peer)[which]
        return remote(src.at[u], dst.at[u], g_send.at[u, which], g_recv.at[u, which], peer)

    def turn(u):
        write_left(u).start()
        for c in range(0, R, 128):
            turned[:, c : c + 128] = final[u, c : c + 128, :].T

        high, low = split(turned[...])
        turned_split[:H, :] = high
        turned_split[H:, :] = low

    def gram_first(u):
        e, h = u // 2, lax.rem(u, 2)

        def block(j, at):
            gram0[u, :, at] = jnp.dot(turned[...], final[e * 2 + j], precision=FULL, preferred_element_type=F32)

        block(0, slice(0, H))
        pl.when(h == 1)(lambda: block(1, slice(H, K)))

        @pl.when(h == 0)
        def _():
            gram0[u, :, H:] = jnp.zeros((H, K - H), F32)

        gram_copy(u, 0).start()

    def gram_second(u):
        gram_copy(u, 0).wait_recv()
        gram_core[u] = gram0[u] + gram_core[u]
        gram_copy(u, 1).start()

    def gram_third(u):
        gram_copy(u, 1).wait_recv()
        gram_x[u] = gram_core[u] + gram_x[u]

    def full(a, b, rows=False):
        if rows:
            return lax.dot_general(a, b, (((1,), (1,)), ((), ())), precision=FULL, preferred_element_type=F32)
        return jnp.dot(a, b, precision=FULL, preferred_element_type=F32)

    def factor_first(u):
        e, h = u // 2, lax.rem(u, 2)
        eye = jnp.where(
            lax.broadcasted_iota(jnp.int32, (H, H), 0) == lax.broadcasted_iota(jnp.int32, (H, H), 1), 1.0, 0.0
        ).astype(F32)
        work[:, H:] = eye

        @pl.when(h == 0)
        def _():
            work[:, :H] = gram_x[u, :, :H]

        @pl.when(h == 1)
        def _():
            top = inverse[e, :H, :H]
            low = full(gram_x[u, :, :H], top, rows=True)
            work[:, :H] = gram_x[u, :, H:] - full(low, low, rows=True)
            inverse[e, H:, :H] = full(low, top)

        eliminate(work, H, 0)

    def factor_second(u):
        e, h = u // 2, lax.rem(u, 2)
        eliminate(work, H, 1)

        @pl.when(h == 0)
        def _():
            inverse[e, :H, :H] = work[:, H:]
            inverse[e, :H, H:] = jnp.zeros((H, K - H), F32)

        @pl.when(h == 1)
        def _():
            bottom = work[:, H:]
            inverse[e, H:, H:] = bottom
            inverse[e, H:, :H] = -full(bottom, inverse[e, H:, :H])

    def right_copy(u, s, which):
        e, h = u // 2, lax.rem(u, 2)
        tile, other = 2 * s + core, 2 * s + 1 - core
        hs = pl.ds(pl.multiple_of(h * H, H), H)
        if which == 0:
            src, dst, peer = own.at[u, other], from_core.at[u, s], c_peer
        elif which == 1:
            src, dst, peer = own.at[u, tile], from_x.at[u, s], x_peer
        else:
            tile = tile if which == 2 else other
            src = dst = right.at[e, tile, hs, :]
            peer, which = c_peer, 2
        return remote(src, dst, r_send.at[u, s, which], r_recv.at[u, s, which], peer)

    def right_forward(u, s):
        right_copy(u, s, 0).wait_recv()
        tile = 2 * s + core
        own[u, tile] = own[u, tile] + from_core[u, s]
        right_copy(u, s, 1).start()

    def right_product(u, s):
        e = u // 2
        for i in range(2):
            at = pl.ds(pl.multiple_of((s * 2 + i) * W, W), W)
            both = dot(turned_split[...], bh[e, :, at])
            own[u, 2 * s + i] = both[:H] + both[H:] + dot(turned_split[:H, :], bl[e, :, at])
        right_copy(u, s, 0).start()

    def right_sums(u):
        e, h = u // 2, lax.rem(u, 2)
        for s in range(T // 2):
            right_copy(u, s, 1).wait_recv()
            tile = 2 * s + core
            right[e, tile, pl.ds(pl.multiple_of(h * H, H), H), :] = own[u, tile] + from_x[u, s]
            right_copy(u, s, 2).start()

    def right_others(u):
        for s in range(T // 2):
            right_copy(u, s, 3).wait_recv()

    def write_fact(e, j):
        return pltpu.make_async_copy(right.at[e, j], fact_out.at[e, j], out_sem.at[e, 2 + j])

    def write_inverse(e):
        return pltpu.make_async_copy(inverse.at[e], inverse_out.at[e], out_sem.at[e, 2 + T])

    def write_square(e):
        return pltpu.make_async_copy(sq_all.at[e], square_out.at[e], out_sem.at[e, 3 + T])

    def square_copy(e, i):
        peer = lax.rem(d + i, plan.dp)
        return remote(sq.at[e], sq_in.at[e, d], s_send.at[e, i - 1], s_recv.at[e, i - 1], (peer, f))

    def square_arrival(e, i):
        source = lax.rem(d + plan.dp - i, plan.dp)
        return remote(sq.at[e], sq_in.at[e, source], s_send.at[e, i - 1], s_recv.at[e, i - 1], (source, f))

    def factors(e):
        write_inverse(e).start()
        for s in range(T // 2):
            right_copy(e * 2, s, 2).wait_send()
            right_copy(e * 2 + 1, s, 2).wait_send()
        x_high, x_low = split(inverse[e])
        total = jnp.zeros((K, 128), F32)
        for j in range(T):
            high, low = split(right[e, j])
            value = dot(x_high, high) + dot(x_low, high) + dot(x_high, low)
            right[e, j] = value
            write_fact(e, j).start()
            for c in range(0, W, 128):
                total = total + value[:, c : c + 128] * value[:, c : c + 128]
        row = jnp.sum(total.T, axis=0, keepdims=True)
        sq[e] = jnp.broadcast_to(row, (8, K))
        for i in range(1, plan.dp):
            square_copy(e, i).start()
        sq_in[e, d] = sq[e]

    def square_sum(e):
        for i in range(1, plan.dp):
            square_arrival(e, i).wait_recv()
        total = sq_in[e, 0]
        for i in range(1, plan.dp):
            total = total + sq_in[e, i]
        sq_all[e] = total
        write_square(e).start()

    left_pair(0)
    pl.semaphore_wait(barrier, plan.dp + 1)
    slot(0)

    def early(t, carry):
        left_pair(t)
        slot(t)
        return carry

    lax.fori_loop(1, E * NP, early, 0)

    FIRST = NP - 1 + DELAYS[-1]
    lax.fori_loop(E * NP, FIRST, lambda t, carry: (slot(t), carry)[1], 0)

    def late(u, carry):
        t = FIRST + u * NP
        slot(t)
        turn(u)
        gram_first(u)
        right_product(u, 0)
        gram_second(u)
        right_product(u, 1)
        right_forward(u, 0)
        slot(t + 1)
        for s in range(2, T // 2):
            right_product(u, s)
            right_forward(u, s - 1)
        slot(t + 2)
        right_forward(u, T // 2 - 1)
        gram_third(u)
        factor_first(u)
        slot(t + 3)
        pl.when(u > 0)(lambda: right_sums(u - 1))
        factor_second(u)

        @pl.when(u == 2)
        def _():
            right_others(0)
            right_others(1)
            factors(0)

        return carry

    lax.fori_loop(0, E * 2, late, 0)
    right_sums(E * 2 - 1)
    right_others(E * 2 - 2)
    right_others(E * 2 - 1)
    factors(E - 1)
    square_sum(0)
    square_sum(E - 1)

    lax.fori_loop(0, SLOTS, lambda k, carry: (drain(k), carry)[1], 0)

    def close(u, carry):
        for s in range(T // 2):
            right_copy(u, s, 0).wait_send()
            right_copy(u, s, 1).wait_send()
        gram_copy(u, 0).wait_send()
        gram_copy(u, 1).wait_send()
        write_left(u).wait()
        return carry

    lax.fori_loop(0, E * 2, close, 0)
    for e in range(E):
        for i in range(1, plan.dp):
            square_copy(e, i).wait_send()
        for j in range(T):
            write_fact(e, j).wait()
        write_inverse(e).wait()
        write_square(e).wait()


def factor_call(plan, momentum, gradient, q_factor):
    E, R, C, K, H = plan.matrices, plan.rows, plan.cols, plan.rank, plan.half_rank
    NP, CH, HF, W, T = plan.pairs, plan.chunk, plan.half, plan.width, plan.tiles
    U = E * 2 * NP
    any_spec = pl.BlockSpec(memory_space=pl.ANY)
    vmem = pltpu.VMEM
    flops = 14 * E * R * C * K
    return pl.pallas_call(
        functools.partial(factor_kernel, plan),
        out_shape=(
            jax.ShapeDtypeStruct((E, 2, R, H), F32),
            jax.ShapeDtypeStruct((E, K, K), F32),
            jax.ShapeDtypeStruct((E, T, K, W), F32),
            jax.ShapeDtypeStruct((E, 8, K), F32),
        ),
        in_specs=[any_spec] * 3,
        out_specs=(any_spec,) * 4,
        scratch_shapes=[
            vmem((E, R, C), BF16),
            vmem((E, R, C), BF16),
            vmem((2, 2 * CH, C // 2), F32),
            vmem((2, 2 * CH, C // 2), BF16),
            vmem((C, K), BF16),
            vmem((C, K), BF16),
            vmem((E * 2, R, H), F32),
            vmem((E * 2, R, H), F32),
            vmem((U, HF, H), F32),
            vmem((U, HF, H), F32),
            vmem((U, HF, H), F32),
            vmem((U, CH, H), F32),
            vmem((U, HF, H), F32),
            vmem((U, HF, H), F32),
            vmem((H, R), F32),
            vmem((K, R), BF16),
            vmem((E * 2, T, H, W), F32),
            vmem((E * 2, T // 2, H, W), F32),
            vmem((E * 2, T // 2, H, W), F32),
            vmem((E, T, K, W), F32),
            vmem((E * 2, H, K), F32),
            vmem((E * 2, H, K), F32),
            vmem((E * 2, H, K), F32),
            vmem((H, K), F32),
            vmem((E, K, K), F32),
            vmem((E, 8, K), F32),
            vmem((E, plan.dp, 8, K), F32),
            vmem((E, 8, K), F32),
            pltpu.SemaphoreType.DMA((2, 2)),
            pltpu.SemaphoreType.DMA((T,)),
            pltpu.SemaphoreType.DMA((U, 9)),
            pltpu.SemaphoreType.DMA((U, 8)),
            pltpu.SemaphoreType.DMA((E * 2, T // 2, 3)),
            pltpu.SemaphoreType.DMA((E * 2, T // 2, 3)),
            pltpu.SemaphoreType.DMA((E * 2, 2)),
            pltpu.SemaphoreType.DMA((E * 2, 2)),
            pltpu.SemaphoreType.DMA((E, plan.dp - 1)),
            pltpu.SemaphoreType.DMA((E, plan.dp - 1)),
            pltpu.SemaphoreType.DMA((E, T + 4)),
        ],
        compiler_params=pltpu.CompilerParams(
            collective_id=0, has_side_effects=True, vmem_limit_bytes=67043328
        ),
        cost_estimate=pl.CostEstimate(flops=flops, bytes_accessed=6 * E * R * C, transcendentals=0),
        name="dion_factors",
    )(momentum, gradient, q_factor)


def output_kernel(
    rms, total_cols, parts, mom, grad, left, inverse, fact, square, new_mom, update, new_q, fh, fl, xh, xl
):
    tiles, width = fact.shape[1], fact.shape[3]
    step = pl.program_id(1)

    @pl.when(step == 0)
    def _():
        for j in range(tiles):
            high, low = split(fact[0, j])
            fh[j] = high
            fl[j] = low
        high, low = split(inverse[0])
        xh[...] = high
        xl[...] = low

    scale = lax.rsqrt(square[0, 0:1, :] / total_cols + epsilon)
    rows = mom.shape[1] // parts

    def piece(i, carry):
        at_rows = pl.ds(pl.multiple_of(i * rows, rows), rows)
        high, low = split(jnp.concatenate([left[0, 0, at_rows, :], left[0, 1, at_rows, :]], axis=1))
        ortho = dot_rows(high, xh[...]) + dot_rows(low, xh[...]) + dot_rows(high, xl[...])
        feed = (ortho * (1.0 - ema_decay)).astype(BF16)
        high, low = split(ortho * (scale * rms))
        stack = jnp.concatenate([feed, high, low], axis=0)
        for j in range(tiles):
            at = slice(j * width, (j + 1) * width)
            value = dot(stack, fh[j])
            direction = value[rows : 2 * rows] + value[2 * rows :] + dot(high, fl[j])
            new_mom[0, at_rows, at] = (mom[0, at_rows, at] + grad[0, at_rows, at].astype(F32)) - value[:rows]
            update[0, at_rows, at] = direction.astype(BF16)
        new_q[0, pl.ds(pl.multiple_of(i * width, width), width), :] = fact[0, step * parts + i].T * scale
        return carry

    lax.fori_loop(0, parts, piece, 0)


def output_call(plan, momentum, gradient, left, inverse, fact, square):
    E, R, C, K, H = plan.matrices, plan.rows, plan.cols, plan.rank, plan.half_rank
    T, W = plan.tiles, plan.width
    parts = 2
    block = R // T * parts
    rms = math.sqrt(R * plan.fsdp / K)
    tall = pl.BlockSpec((1, block, C), lambda e, i: (e, i, 0))
    return pl.pallas_call(
        functools.partial(output_kernel, rms, float(C * plan.dp), parts),
        grid=(E, T // parts),
        out_shape=(
            jax.ShapeDtypeStruct((E, R, C), F32),
            jax.ShapeDtypeStruct((E, R, C), BF16),
            jax.ShapeDtypeStruct((E, C, K), F32),
        ),
        in_specs=[
            tall,
            tall,
            pl.BlockSpec((1, 2, block, H), lambda e, i: (e, 0, i, 0)),
            pl.BlockSpec((1, K, K), lambda e, i: (e, 0, 0)),
            pl.BlockSpec((1, T, K, W), lambda e, i: (e, 0, 0, 0)),
            pl.BlockSpec((1, 8, K), lambda e, i: (e, 0, 0)),
        ],
        out_specs=(tall, tall, pl.BlockSpec((1, W * parts, K), lambda e, i: (e, i, 0))),
        scratch_shapes=[
            pltpu.VMEM((T, K, W), BF16),
            pltpu.VMEM((T, K, W), BF16),
            pltpu.VMEM((K, K), BF16),
            pltpu.VMEM((K, K), BF16),
        ],
        compiler_params=pltpu.CompilerParams(vmem_limit_bytes=67043328),
        cost_estimate=pl.CostEstimate(
            flops=8 * E * R * C * K, bytes_accessed=12 * E * R * C, transcendentals=0
        ),
        name="dion_outputs",
    )(momentum, gradient, left, inverse, fact, square)


def body(mesh, momentum, gradient, q_factor):
    plan = Plan(mesh, momentum, q_factor)
    if not plan.fits():
        return general_body(momentum, gradient, q_factor)
    left, inverse, fact, square = factor_call(plan, momentum, gradient, q_factor)
    return output_call(plan, momentum, gradient, left, inverse, fact, square)


def solution(mesh):
    placed = (P(None, "fsdp", "dp"), P(None, "fsdp", "dp"), P(None, "dp", None))
    return jax.shard_map(
        functools.partial(body, mesh),
        mesh=mesh,
        in_specs=placed,
        out_specs=(P(None, "fsdp", "dp"), P(None, "fsdp", "dp"), P(None, "dp", None)),
        check_vma=False,
    )
```

time: 207 us -> 161 us (0.78); the launches traced: 207 us -> 158 us
  Pallas kernels: 202 us -> 157 us
  local copies, waits for them, and re-layouts: 3.64 us -> 0 us
    pallas_call x1, Pallas kernels: 165 us -> 119 us  [factor_call(): pl.pallas_call(functools.partial(factor_kernel, plan), out_shape=(jax.Sha...]
    unnamed x6 -> x0, local copies, waits for them, and re-layouts: 3.64 us -> none
where the time goes in v1:
time: 161 us; the launch traced here: 158 us
  Pallas kernels  157 us (98%)
    pallas_call x1, Pallas kernels, factor_call(): pl.pallas_call(functools.partial(factor_kernel, plan), out_shape=(jax.Sha...  119 us
    pallas_call x1, Pallas kernels, output_call(): pl.pallas_call(functools.partial(output_kernel, rms, float(C * plan.dp),...  38.7 us

profile of v1, /device:TPU:12, one launch (start us, length us, event | category | flops | bytes accessed | tf_op | source)
XLA Modules:
  0.0 157.8 jit_solution(11863182423244092982)
XLA Ops:
  0.6 118.5 %dion_factors.1 = (f32[2,2,1536,128]{3,2,1,0:T(8,128)}, f32[2,256,256]{2,1,0:T(8,128)}, f32[2,8,256,256]{3,2,1,0:T(8,128)}, f32[2,8,256]{2,1,0:T(8,128)}) custom-call(f32[2,1536,2048]{2,1,0:T(8,128)} %mom.3, bf16[2,1536,2048]{2,1,0:T(8,128)(2,1)} %grad.3, f32[2,2048,256]{2,1,0:T(8,128)} %q.1), custom_call_target="tpu_custom_call" | custom-call | flops 22548578304 | bytes 37748736 | tf_op jit(solution)/shard_map/dion_factors/pallas_call | solution.py:742
  119.2 38.7 %dion_outputs.1 = (f32[2,1536,2048]{2,1,0:T(8,128)}, bf16[2,1536,2048]{2,1,0:T(8,128)(2,1)}, f32[2,2048,256]{2,1,0:T(8,128)}) custom-call(f32[2,1536,2048]{2,1,0:T(8,128)} %mom.3, bf16[2,1536,2048]{2,1,0:T(8,128)(2,1)} %grad.3, f32[2,2,1536,128]{3,2,1,0:T(8,128)} %get-tuple-element.7.left, f32[2,256,256]{2,1,0:T(8,128)} %get-tuple-element.8.inverse, ...), custom_call_target="tpu_custom_call" | custom-call | flops 12884901888 | bytes 75497472 | tf_op jit(solution)/shard_map/dion_outputs/pallas_call | solution.py:846
